TPU v7x, 32 devices: a whole 2x2x4 slice. The times are simulated.
32 devices in a mesh: rows: 8 (over z, y), grp: 4 (over x, core).
Axes of the slice: x: 2, y: 2, z: 4, core: 2. Of those that a mesh axis runs over, the one named last changes fastest.
Arguments:
- activations: bfloat16 [3072, 2048], P(('rows', 'grp')), may hold values from 0 to 1
- weight_tiles: bfloat16 [3, 512, 2, 128, 128], P(None, ('rows', 'grp')), may hold values from -0.75 to 0.75
- tile_index: int32 [3, 512, 1], replicated, may hold values from 0 to 511, as said below
- bias_terms: float32 [3, 65536], replicated, may hold values from -0.3 to 0.3
- demand: int32 [32, 16], P(('rows', 'grp')), may hold values from 0 to 511, as said below
Outputs:
- final_acts: bfloat16 [3072, 2048], P(('rows', 'grp'))
Inputs may be any that keep to these rules, and one draw needn't show every extreme that they name: Each row of demand lists 16 distinct blocks made of whole groups [g * 4, (g + 1) * 4); every range [r * 64, (r + 1) * 64) holds either none of them or exactly one group of 4. tile_index[l, b, k] is a block of b's own group [(b // 4) * 4, (b // 4 + 1) * 4), never b itself.
All inputs are finite; a program needn't handle non-finite values.
Results may differ from a plain program's by a relative error of at most 0.0057.
Values may be sent and summed in bfloat16 or wider, within the bound.
A program may use at most 128 MiB of HBM per device.

v0:
```python
import functools

import jax
import jax.numpy as jnp
from jax import lax
from jax.experimental import pallas as pl
from jax.experimental.pallas import tpu as pltpu
from jax.sharding import PartitionSpec as P

CAP = 4
CORES = 2
PLANES = 2
LAG = 3
BACK = 2
MESH = pl.DeviceIdType.MESH


def group_step(state, weights, matches, bias_rows):
    chosen = jnp.einsum(
        "sckp,srpt->srckt", matches, state, preferred_element_type=jnp.float32
    ).astype(jnp.bfloat16)
    diag_part = jnp.einsum(
        "srct,sctu->srcu", state, weights[:, :, 0], preferred_element_type=jnp.float32
    )
    off_part = jnp.einsum(
        "srckt,scktu->srcu", chosen, weights[:, :, 1:], preferred_element_type=jnp.float32
    )
    return jax.nn.relu(diag_part + off_part + bias_rows[:, None]).astype(jnp.bfloat16)


def gathered_shards(activations, weight_tiles, tile_index, bias_terms, demand):
    live_blocks = demand[0]
    live_count = live_blocks.shape[0]
    tile_width = weight_tiles.shape[-1]
    row_count = lax.axis_size("rows")
    per_range = weight_tiles.shape[1] * lax.axis_size("grp")
    owners = live_blocks // per_range
    within = live_blocks % per_range
    range_ids = jnp.arange(row_count, dtype=jnp.int32)
    slot_ids = jnp.arange(CAP, dtype=jnp.int32)
    current = activations.reshape(activations.shape[0], live_count, tile_width)
    bias_blocks = bias_terms.reshape(bias_terms.shape[0], -1, tile_width)
    grouped = lax.all_gather(weight_tiles, "grp", axis=1, tiled=True)
    member = live_blocks % CAP
    placing = (owners[None, None, :] == range_ids[:, None, None]) & (
        member[None, None, :] == slot_ids[None, :, None]
    )
    starts = jnp.sum(placing[:, 0, :].astype(jnp.int32) * (within[None, :] + 1), axis=1) - 1
    outgoing = jnp.einsum(
        "acp,rpt->arct", placing.astype(jnp.bfloat16), current, preferred_element_type=jnp.float32
    ).astype(jnp.bfloat16)
    arrived = lax.all_to_all(outgoing, "rows", split_axis=0, concat_axis=0, tiled=True)
    bases = lax.all_to_all(
        starts.reshape(row_count, 1), "rows", split_axis=0, concat_axis=0, tiled=True
    )[:, 0]
    slot_blocks = jnp.clip(bases, 0)[:, None] + slot_ids[None, :]
    global_blocks = lax.axis_index("rows") * per_range + slot_blocks
    state = arrived
    for layer_num in range(weight_tiles.shape[0]):
        weights = grouped[layer_num][slot_blocks]
        off_member = tile_index[layer_num][global_blocks] % CAP
        matches = (off_member[:, :, :, None] == slot_ids[None, None, None, :]).astype(jnp.bfloat16)
        state = group_step(state, weights, matches, bias_blocks[layer_num][global_blocks])
    returned = lax.all_to_all(state, "rows", split_axis=0, concat_axis=0, tiled=True)
    current = jnp.einsum(
        "acp,arct->rpt", placing.astype(jnp.bfloat16), returned, preferred_element_type=jnp.float32
    ).astype(jnp.bfloat16)
    return current.reshape(current.shape[0], live_count * tile_width)


def fused_kernel(
    n, pos_ref, home_ref, index_ref, meta_ref, act_ref, bias_ref, w_hbm, out_ref,
    w_all, slots, zin, xin, ores, fres, xres, sel, fin, st_own, st_for, meta_in, meta_s,
    w_sems, m_send, m_recv, m_copy, z_send, z_recv, x_send, x_recv,
    b_send, b_recv, f_send, f_recv,
):
    layers, held = w_hbm.shape[0], w_hbm.shape[1]
    tile = w_hbm.shape[-1]
    live = home_ref.shape[1]
    r = lax.axis_index("rows")
    g = lax.axis_index("grp")
    plane, core = g // CORES, g % CORES
    mate = plane * CORES + (CORES - 1 - core)
    cross = (PLANES - 1 - plane) * CORES + core

    def up(k):
        return lax.rem(r + k, n)

    def down(k):
        return lax.rem(r - k + n, n)

    barrier = pltpu.get_barrier_semaphore()
    pl.semaphore_signal(barrier, inc=1, device_id=(r, mate), device_id_type=MESH)

    def greet(k, carry):
        pl.semaphore_signal(barrier, inc=1, device_id=(up(k), g), device_id_type=MESH)
        pl.semaphore_signal(barrier, inc=1, device_id=(up(k), cross), device_id_type=MESH)
        return carry

    lax.fori_loop(1, n, greet, 0)
    pl.semaphore_signal(barrier, inc=1, device_id=(r, cross), device_id_type=MESH)

    w_local = pltpu.make_async_copy(w_hbm, w_all.at[core], w_sems.at[0])
    w_local.start()
    for a in range(n):
        for c in range(CAP):
            slots[a, c] = act_ref[pos_ref[a, c]]
    meta_in[0, r] = meta_ref[r]
    pl.semaphore_wait(barrier, 2 * n)

    def meta_copy(which, slot, row, dev_row, dev_grp):
        return pltpu.make_async_remote_copy(
            src_ref=meta_ref.at[row], dst_ref=meta_in.at[which, slot],
            send_sem=m_send.at[which, row], recv_sem=m_recv.at[which, slot],
            device_id=(dev_row, dev_grp), device_id_type=MESH,
        )

    def z_copy(row, slot):
        return pltpu.make_async_remote_copy(
            src_ref=slots.at[row], dst_ref=zin.at[slot],
            send_sem=z_send.at[row], recv_sem=z_recv.at[slot],
            device_id=(row, g), device_id_type=MESH,
        )

    def x_copy(src, slot):
        return pltpu.make_async_remote_copy(
            src_ref=src.at[slot], dst_ref=xin.at[slot],
            send_sem=x_send.at[slot], recv_sem=x_recv.at[slot],
            device_id=(r, cross), device_id_type=MESH,
        )

    def b_copy(slot):
        return pltpu.make_async_remote_copy(
            src_ref=fres.at[slot], dst_ref=xres.at[slot],
            send_sem=b_send.at[slot], recv_sem=b_recv.at[slot],
            device_id=(r, cross), device_id_type=MESH,
        )

    def f_copy(row, slot):
        return pltpu.make_async_remote_copy(
            src_ref=sel.at[row], dst_ref=fin.at[slot],
            send_sem=f_send.at[row], recv_sem=f_recv.at[slot],
            device_id=(row, g), device_id_type=MESH,
        )

    w_remote = pltpu.make_async_remote_copy(
        src_ref=w_hbm, dst_ref=w_all.at[core],
        send_sem=w_sems.at[1], recv_sem=w_sems.at[2],
        device_id=(r, mate), device_id_type=MESH,
    )
    w_arrives = pltpu.make_async_remote_copy(
        src_ref=w_hbm, dst_ref=w_all.at[CORES - 1 - core],
        send_sem=w_sems.at[1], recv_sem=w_sems.at[2],
        device_id=(r, mate), device_id_type=MESH,
    )

    def send_meta(k, carry):
        row = up(k)
        meta_copy(0, r, row, row, g).start()
        meta_copy(1, r, row, row, cross).start()
        return carry

    x_copy(slots, r).start()
    meta_copy(1, r, r, r, cross).start()
    lax.fori_loop(1, n, send_meta, 0)

    def send_rows(k, carry):
        z_copy(up(k), r).start()
        return carry

    lax.fori_loop(1, n, send_rows, 0)
    w_remote.start()

    def forward(k):
        slot = down(k)
        z_copy(r, slot).wait_recv()
        x_copy(zin, slot).start()

    for k in range(1, min(LAG, n)):
        forward(k)
    meta_copy(1, r, r, r, cross).wait_recv()

    def take_meta(k, carry):
        meta_copy(0, down(k), r, r, g).wait_recv()
        meta_copy(1, down(k), r, r, cross).wait_recv()
        return carry

    lax.fori_loop(1, n, take_meta, 0)
    to_smem = pltpu.make_async_copy(meta_in, meta_s, m_copy)
    to_smem.start()
    to_smem.wait()
    w_local.wait()
    w_arrives.wait_recv()

    def compute(jobs):
        for load, slot, _, state, _ in jobs:
            for j in range(CAP):
                state[0, j] = load[slot, j]
        for layer in range(layers):
            for _, slot, store, state, which in jobs:
                half = meta_s[which, slot, 0, 0]
                local = meta_s[which, slot, 0, 1]
                inner = meta_s[which, slot, 0, 2]
                for j in range(CAP):
                    other = index_ref[layer, inner + j]
                    pair = (state[layer % 2, j], state[layer % 2, other])
                    pre = jnp.dot(
                        jnp.concatenate(pair, axis=1), w_all[half, layer, local + j],
                        preferred_element_type=jnp.float32,
                    ) + bias_ref[layer, inner + j]
                    value = jnp.maximum(pre, 0.0).astype(jnp.bfloat16)
                    if layer == layers - 1:
                        store[slot, j] = value
                    else:
                        state[(layer + 1) % 2, j] = value

    def step(k, own_buf):
        slot = down(k)
        x_copy(zin, slot).wait_recv()
        compute((
            (xin, slot, fres, st_for, 1),
            (own_buf, slot, ores, st_own, 0),
        ))
        b_copy(slot).start()

    def choose(slot):
        b_copy(slot).wait_recv()
        mine = (meta_s[0, slot, 0, 3] == plane).astype(jnp.float32)
        for j in range(CAP):
            sel[slot, j] = (
                ores[slot, j].astype(jnp.float32) * mine
                + xres[slot, j].astype(jnp.float32) * (1.0 - mine)
            ).astype(jnp.bfloat16)

    def send_back(k, carry):
        slot = down(k)
        choose(slot)
        f_copy(slot, r).start()
        return carry

    forward(LAG)
    step(0, slots)

    def first(k, carry):
        forward(k + LAG)
        step(k, zin)
        return carry

    def middle(k, carry):
        forward(k + LAG)
        step(k, zin)
        return send_back(k - BACK, carry)

    def late(k, carry):
        step(k, zin)
        return send_back(k - BACK, carry)

    lax.fori_loop(1, BACK + 1, first, 0)
    choose(r)
    lax.fori_loop(BACK + 1, n - LAG, middle, 0)
    lax.fori_loop(n - LAG, n, late, 0)
    lax.fori_loop(n - BACK, n, send_back, 0)

    def take(k, carry):
        f_copy(r, down(k)).wait_recv()
        return carry

    lax.fori_loop(1, n, take, 0)
    fin[r] = sel[r]
    for p in range(live):
        out_ref[:, p * tile:(p + 1) * tile] = fin[home_ref[0, p], home_ref[1, p]]

    def drain(k, carry):
        row = up(k)
        meta_copy(0, r, row, row, g).wait_send()
        meta_copy(1, r, row, row, cross).wait_send()
        z_copy(row, r).wait_send()
        x_copy(zin, row).wait_send()
        b_copy(row).wait_send()
        f_copy(row, r).wait_send()
        return carry

    lax.fori_loop(1, n, drain, 0)
    meta_copy(1, r, r, r, cross).wait_send()
    x_copy(slots, r).wait_send()
    b_copy(r).wait_send()
    w_remote.wait_send()


def fused_shards(activations, weight_tiles, tile_index, bias_terms, demand):
    n = lax.axis_size("rows")
    layers, held, kinds, tile, _ = weight_tiles.shape
    per_range = held * lax.axis_size("grp")
    depth = activations.shape[0]
    blocks = demand[0]
    owners, within, member = blocks // per_range, blocks % per_range, blocks % CAP
    placing = (owners[None, None, :] == jnp.arange(n, dtype=jnp.int32)[:, None, None]) & (
        member[None, None, :] == jnp.arange(CAP, dtype=jnp.int32)[None, :, None]
    )
    places = jnp.arange(blocks.shape[0], dtype=jnp.int32)
    pos = jnp.sum(jnp.where(placing, places, 0), axis=2)
    starts = jnp.sum(jnp.where(placing[:, 0], within, 0), axis=1)
    chip_blocks = held * CORES
    inner = starts % chip_blocks
    facts = jnp.stack([inner // held, inner % held, inner, starts // chip_blocks], axis=1)
    meta = jnp.pad(facts, ((0, 0), (0, 124)))[:, None, :]
    home = jnp.stack([owners, member])
    chip = (lax.axis_index("rows") * PLANES + lax.axis_index("grp") // CORES) * chip_blocks
    others = lax.dynamic_slice_in_dim(tile_index[:, :, 0], chip, chip_blocks, axis=1) % CAP
    bias = lax.dynamic_slice_in_dim(bias_terms, chip * tile, chip_blocks * tile, axis=1)
    bias = bias.reshape(layers, chip_blocks, 1, tile)
    weights = weight_tiles.reshape(layers, held, kinds * tile, tile)
    columns = activations.reshape(depth, blocks.shape[0], tile).transpose(1, 0, 2)
    smem = pl.BlockSpec(memory_space=pltpu.SMEM)
    vmem = pl.BlockSpec(memory_space=pltpu.VMEM)
    slot = pltpu.VMEM((n, CAP, depth, tile), jnp.bfloat16)
    sems = pltpu.SemaphoreType.DMA((n,))
    return pl.pallas_call(
        functools.partial(fused_kernel, n),
        out_shape=jax.ShapeDtypeStruct(activations.shape, jnp.bfloat16),
        in_specs=[smem, smem, smem, vmem, vmem, vmem, pl.BlockSpec(memory_space=pl.ANY)],
        out_specs=vmem,
        scratch_shapes=[
            pltpu.VMEM((CORES, layers, held, kinds * tile, tile), jnp.bfloat16),
            slot, slot, slot, slot, slot, slot, slot, slot,
            pltpu.VMEM((2, CAP, depth, tile), jnp.bfloat16),
            pltpu.VMEM((2, CAP, depth, tile), jnp.bfloat16),
            pltpu.VMEM((2, n, 1, 128), jnp.int32),
            pltpu.SMEM((2, n, 1, 128), jnp.int32),
            pltpu.SemaphoreType.DMA((3,)),
            pltpu.SemaphoreType.DMA((2, n)),
            pltpu.SemaphoreType.DMA((2, n)),
            pltpu.SemaphoreType.DMA,
            sems, sems, sems, sems, sems, sems, sems, sems,
        ],
        compiler_params=pltpu.CompilerParams(
            collective_id=0, has_side_effects=True, vmem_limit_bytes=40 * 1024 * 1024
        ),
    )(pos, home, others, meta, columns, bias, weights)


def solution(mesh):
    def shards(activations, weight_tiles, tile_index, bias_terms, demand):
        whole_groups = weight_tiles.shape[1] % CAP == 0 and weight_tiles.shape[2] == 2
        if whole_groups and mesh.shape["grp"] == PLANES * CORES and mesh.shape["rows"] > LAG + BACK:
            return fused_shards(activations, weight_tiles, tile_index, bias_terms, demand)
        return gathered_shards(activations, weight_tiles, tile_index, bias_terms, demand)

    return jax.shard_map(
        shards,
        mesh=mesh,
        in_specs=(
            P(("rows", "grp"), None),
            P(None, ("rows", "grp"), None, None, None),
            P(),
            P(),
            P(("rows", "grp"), None),
        ),
        out_specs=P(("rows", "grp"), None),
        check_vma=False,
    )
```

profile of v0, /device:TPU:0, one launch (start us, length us, event | category | flops | bytes accessed | tf_op | source)
XLA Modules:
  0.0 63.8 jit_solution(7080102079083713177)
XLA Ops:
  0.0 0.0 copy-start
  0.0 0.8 %constant_dynamic-slice_fusion.1 = s32[3,32,1]{1,2,0:T(1,128)S(1)} fusion(s32[3,512,1]{1,2,0:T(1,128)} %param.7, s32[]{:T(128)S(6)} %select_n.114), kind=kLoop, calls=%fused_computation.45 | loop fusion | bytes 772 | tf_op jit(solution)/shard_map/dynamic_slice | solution.py:309
  0.9 0.7 %and_select_fusion.2 = (s32[1,16]{1,0:T(1,128)S(1)}, s32[1,16]{1,0:T(1,128)S(1)}) fusion(s32[1,16]{1,0:T(1,128)} %param.9), kind=kLoop, calls=%fused_computation.30 | loop fusion | flops 368 | bytes 192 | tf_op jit(solution)/shard_map/jit(floor_divide)/jit(_where)/select_n | solution.py:296
  1.5 0.7 %and_select_fusion = (s32[16]{0:T(128)S(1)}, s32[16]{0:T(128)S(1)}, s32[16]{0:T(128)S(1)}) fusion(s32[1,16]{1,0:T(1,128)} %param.9), kind=kLoop, calls=%fused_computation.28 | loop fusion | flops 432 | bytes 256 | tf_op jit(solution)/shard_map/jit(remainder)/select_n | solution.py:296
  2.2 0.1 select_reduce_fusion
  2.4 0.1 copy.20.pos_ref
  2.5 0.1 select_reduce_fusion.1
  2.6 0.1 copy.15
  2.7 0.1 pad_add_fusion
  2.8 0.0 copy-done
  2.8 0.1 reshape.250.bias_ref
  2.9 1.1 %bitcast_bitcast_fusion.act_ref = bf16[16,96,128]{2,1,0:T(8,128)(2,1)S(1)} fusion(bf16[96,2048]{1,0:T(8,128)(2,1)} %param.5), kind=kLoop, calls=%fused_computation | loop fusion | bytes 786432 | tf_op jit(solution)/shard_map/transpose | solution.py:313
  4.0 0.0 copy-start.1
  4.0 1.9 %copy-done.1 = bf16[3,16,2,128,128]{4,3,2,1,0:T(8,128)(2,1)S(1)} copy-done((bf16[3,16,2,128,128]{4,3,2,1,0:T(8,128)(2,1)S(1)}, bf16[3,16,2,128,128]{4,3,2,1,0:T(8,128)(2,1)}, u32[]{:S(2)}) %copy-start.1) | copy-done | bytes 3145752
  5.9 57.2 %shard_map.55 = bf16[96,2048]{1,0:T(8,128)(2,1)S(1)} custom-call(s32[8,4]{1,0:T(8,128)S(1)} %copy.20.pos_ref, s32[2,16]{1,0:T(2,128)S(1)} %pad_add_fusion.1.home_ref, s32[3,32]{1,0:T(4,128)S(1)} %add_select_fusion.4.index_ref, s32[8,1,128]{2,1,0:T(1,128)S(1)} %bitcast.43, bf16[16,96,128]{2,1,0:T(8,128)(2,1)S(1)} %bitcast_bitcast_fusion.act_ref, ...), custom_call_target="tpu_custom_call" | custom-call | tf_op jit(solution)/shard_map/pallas_call | solution.py:318
  63.0 0.7 %copy.28 = bf16[96,2048]{1,0:T(8,128)(2,1)} copy(bf16[96,2048]{1,0:T(8,128)(2,1)S(1)} %shard_map.55) | data formatting | bytes 786432
  (8 shorter events, 0.1 us)
Async XLA Ops:
  0.0 2.8 %copy-start = (f32[3,65536]{1,0:T(4,128)S(1)}, f32[3,65536]{1,0:T(4,128)}, u32[]{:S(2)}) copy-start(f32[3,65536]{1,0:T(4,128)} %param.8) | copy-start | bytes 2359300
  4.0 1.9 %copy-start.1 = (bf16[3,16,2,128,128]{4,3,2,1,0:T(8,128)(2,1)S(1)}, bf16[3,16,2,128,128]{4,3,2,1,0:T(8,128)(2,1)}, u32[]{:S(2)}) copy-start(bf16[3,16,2,128,128]{4,3,2,1,0:T(8,128)(2,1)} %param.6) | copy-start | bytes 9437188
where the time goes:
time: 64 us; the launch traced here: 63.8 us
  Pallas kernels  57.2 us (89%)
  local copies, waits for them, and re-layouts  4.81 us (8%)
  other arithmetic  1.74 us (3%)
    pallas_call x1, Pallas kernels, fused_shards(): pl.pallas_call(functools.partial(fused_kernel, n), out_shape=jax.ShapeDty...  57.2 us
    unnamed x5, local copies, waits for them, and re-layouts  2.64 us

commit v1 on v0

v1 whole, which is shorter than its diff:
```python
import functools

import jax
import jax.numpy as jnp
from jax import lax
from jax.experimental import pallas as pl
from jax.experimental.pallas import tpu as pltpu
from jax.sharding import PartitionSpec as P

CAP = 4
CORES = 2
PLANES = 2
SENDS = (1, 2, 3, 6, 4, 7, 5)
MESH = pl.DeviceIdType.MESH


def group_step(state, weights, matches, bias_rows):
    chosen = jnp.einsum(
        "sckp,srpt->srckt", matches, state, preferred_element_type=jnp.float32
    ).astype(jnp.bfloat16)
    diag_part = jnp.einsum(
        "srct,sctu->srcu", state, weights[:, :, 0], preferred_element_type=jnp.float32
    )
    off_part = jnp.einsum(
        "srckt,scktu->srcu", chosen, weights[:, :, 1:], preferred_element_type=jnp.float32
    )
    return jax.nn.relu(diag_part + off_part + bias_rows[:, None]).astype(jnp.bfloat16)


def gathered_shards(activations, weight_tiles, tile_index, bias_terms, demand):
    live_blocks = demand[0]
    live_count = live_blocks.shape[0]
    tile_width = weight_tiles.shape[-1]
    row_count = lax.axis_size("rows")
    per_range = weight_tiles.shape[1] * lax.axis_size("grp")
    owners = live_blocks // per_range
    within = live_blocks % per_range
    range_ids = jnp.arange(row_count, dtype=jnp.int32)
    slot_ids = jnp.arange(CAP, dtype=jnp.int32)
    current = activations.reshape(activations.shape[0], live_count, tile_width)
    bias_blocks = bias_terms.reshape(bias_terms.shape[0], -1, tile_width)
    grouped = lax.all_gather(weight_tiles, "grp", axis=1, tiled=True)
    member = live_blocks % CAP
    placing = (owners[None, None, :] == range_ids[:, None, None]) & (
        member[None, None, :] == slot_ids[None, :, None]
    )
    starts = jnp.sum(placing[:, 0, :].astype(jnp.int32) * (within[None, :] + 1), axis=1) - 1
    outgoing = jnp.einsum(
        "acp,rpt->arct", placing.astype(jnp.bfloat16), current, preferred_element_type=jnp.float32
    ).astype(jnp.bfloat16)
    arrived = lax.all_to_all(outgoing, "rows", split_axis=0, concat_axis=0, tiled=True)
    bases = lax.all_to_all(
        starts.reshape(row_count, 1), "rows", split_axis=0, concat_axis=0, tiled=True
    )[:, 0]
    slot_blocks = jnp.clip(bases, 0)[:, None] + slot_ids[None, :]
    global_blocks = lax.axis_index("rows") * per_range + slot_blocks
    state = arrived
    for layer_num in range(weight_tiles.shape[0]):
        weights = grouped[layer_num][slot_blocks]
        off_member = tile_index[layer_num][global_blocks] % CAP
        matches = (off_member[:, :, :, None] == slot_ids[None, None, None, :]).astype(jnp.bfloat16)
        state = group_step(state, weights, matches, bias_blocks[layer_num][global_blocks])
    returned = lax.all_to_all(state, "rows", split_axis=0, concat_axis=0, tiled=True)
    current = jnp.einsum(
        "acp,arct->rpt", placing.astype(jnp.bfloat16), returned, preferred_element_type=jnp.float32
    ).astype(jnp.bfloat16)
    return current.reshape(current.shape[0], live_count * tile_width)


SCHEDULE = "F1 F2 F3 M W C0 C1 F4 C2 C3 R0 F5 R1 C4 R2 F6 R3 C5 F7 C6 R4 C7 R5 R6 R7"


def fused_kernel(
    n, demand_ref, index_ref, act_hbm, bias_hbm, w_hbm, out_ref,
    act, bias_in, bias, w_all, slots, zin, xin, ores, fres, xres, sel, fin, st_own, st_for,
    meta_out, meta_in, meta_s, in_sems, w_sems, m_send, m_recv, mx_sems, m_copy,
    z_send, z_recv, x_send, x_recv, b_send, b_recv, f_send, f_recv,
):
    layers, held = w_hbm.shape[0], w_hbm.shape[1]
    tile = w_hbm.shape[-1]
    live = demand_ref.shape[1]
    chip_blocks = held * CORES
    per_range = chip_blocks * PLANES
    r = lax.axis_index("rows")
    g = lax.axis_index("grp")
    plane, core = g // CORES, g % CORES
    mate = plane * CORES + (CORES - 1 - core)
    cross = (PLANES - 1 - plane) * CORES + core
    bits = n.bit_length() - 1

    def peer(k):
        row = 0
        for b in range(bits):
            row = row + ((r // (1 << b)) % 2 + (k >> b)) % 2 * (1 << b)
        return row

    peers = [peer(k) for k in range(n)]
    barrier = pltpu.get_barrier_semaphore()
    for k in range(n - 1, 0, -1):
        pl.semaphore_signal(barrier, inc=1, device_id=(peers[k], g), device_id_type=MESH)
    pl.semaphore_signal(barrier, inc=1, device_id=(r, cross), device_id_type=MESH)
    pl.semaphore_signal(barrier, inc=1, device_id=(r, mate), device_id_type=MESH)

    for p in range(live):
        pltpu.make_async_copy(
            act_hbm.at[:, pl.ds(p * tile, tile)], act.at[p], in_sems.at[0]
        ).start()
    act_copy = pltpu.make_async_copy(act, act, in_sems.at[0])
    first = (r * PLANES + plane) * chip_blocks
    bias_copy = pltpu.make_async_copy(
        bias_hbm.at[:, pl.ds(pl.multiple_of(first * tile, tile), chip_blocks * tile)],
        bias_in, in_sems.at[1],
    )
    bias_copy.start()
    w_local = pltpu.make_async_copy(w_hbm, w_all.at[core], w_sems.at[0])
    w_local.start()

    places = [jnp.int32(0)] * CAP
    groups = jnp.int32(0)
    for p in range(live):
        block = demand_ref[0, p]
        owner = lax.div(block, per_range)
        scale = jnp.int32(1)
        for b in range(bits):
            scale = scale * jnp.where(lax.rem(lax.div(owner, 1 << b), 2) == 1, 1 << (4 << b), 1)
        member = lax.rem(block, CAP)
        for c in range(CAP):
            places[c] = places[c] + jnp.where(member == c, p * scale, 0)
        group = lax.div(lax.rem(block, per_range), CAP)
        groups = groups + jnp.where(member == 0, group * scale, 0)
    meta_out[...] = jnp.full(meta_out.shape, groups, jnp.int32)
    meta_in[0, 0] = jnp.full(meta_out.shape, groups, jnp.int32)
    act_copy.wait()
    for k in range(n - 1, -1, -1):
        for c in range(CAP):
            pos = lax.bitwise_and(lax.shift_right_logical(places[c], peers[k] * 4), 15)
            slots[k, c] = act[pos]

    pl.semaphore_wait(barrier, n + 1)

    def meta_copy(k):
        return pltpu.make_async_remote_copy(
            src_ref=meta_out, dst_ref=meta_in.at[0, k],
            send_sem=m_send.at[k], recv_sem=m_recv.at[k],
            device_id=(peers[k], g), device_id_type=MESH,
        )

    meta_cross = pltpu.make_async_remote_copy(
        src_ref=meta_in.at[0], dst_ref=meta_in.at[1],
        send_sem=mx_sems.at[0], recv_sem=mx_sems.at[1],
        device_id=(r, cross), device_id_type=MESH,
    )

    def z_copy(k):
        return pltpu.make_async_remote_copy(
            src_ref=slots.at[k], dst_ref=zin[k],
            send_sem=z_send.at[k], recv_sem=z_recv.at[k],
            device_id=(peers[k], g), device_id_type=MESH,
        )

    def x_copy(k):
        return pltpu.make_async_remote_copy(
            src_ref=zin[k] if k else slots.at[0], dst_ref=xin[k],
            send_sem=x_send.at[k], recv_sem=x_recv.at[k],
            device_id=(r, cross), device_id_type=MESH,
        )

    def b_copy(k):
        return pltpu.make_async_remote_copy(
            src_ref=fres.at[k], dst_ref=xres.at[k],
            send_sem=b_send.at[k], recv_sem=b_recv.at[k],
            device_id=(r, cross), device_id_type=MESH,
        )

    def f_copy(k):
        return pltpu.make_async_remote_copy(
            src_ref=sel.at[k], dst_ref=fin.at[k],
            send_sem=f_send.at[k], recv_sem=f_recv.at[k],
            device_id=(peers[k], g), device_id_type=MESH,
        )

    w_remote = pltpu.make_async_remote_copy(
        src_ref=w_hbm, dst_ref=w_all.at[core],
        send_sem=w_sems.at[1], recv_sem=w_sems.at[2],
        device_id=(r, mate), device_id_type=MESH,
    )
    w_arrives = pltpu.make_async_remote_copy(
        src_ref=w_hbm, dst_ref=w_all.at[CORES - 1 - core],
        send_sem=w_sems.at[1], recv_sem=w_sems.at[2],
        device_id=(r, mate), device_id_type=MESH,
    )

    for k in SENDS:
        meta_copy(k).start()
    x_copy(0).start()
    for k in SENDS:
        z_copy(k).start()
    w_remote.start()

    def facts(which, k):
        group = lax.bitwise_and(lax.shift_right_logical(meta_s[which, k, 0, 0], r * 4), 15)
        within = group * CAP
        half = lax.rem(within, chip_blocks) // held
        return lax.div(within, chip_blocks), half, lax.rem(within, held), lax.rem(within, chip_blocks)

    def compute(k):
        near = zin[k] if k else slots.at[0]
        jobs = []
        for which, load, store, state in ((1, xin[k], fres, st_for), (0, near, ores, st_own)):
            _, half, local, inner = facts(which, k)
            jobs.append((load, store, state, half, local, inner))
        for layer in range(layers):
            for load, store, state, half, local, inner in jobs:
                for j in range(CAP):
                    other = lax.rem(index_ref[layer, 0, first + inner + j], CAP)
                    if layer == 0:
                        pair = (load[j], load[other])
                    else:
                        pair = (state[layer % 2, j], state[layer % 2, other])
                    pre = jnp.dot(
                        jnp.concatenate(pair, axis=1), w_all[half, layer, local + j],
                        preferred_element_type=jnp.float32,
                    ) + bias[inner + j][layer:layer + 1]
                    value = jnp.maximum(pre, 0.0).astype(jnp.bfloat16)
                    if layer == layers - 1:
                        store[k, j] = value
                    else:
                        state[(layer + 1) % 2, j] = value

    for token in SCHEDULE.split():
        op, k = token[0], int(token[1:] or 0)
        if op == "F":
            z_copy(k).wait_recv()
            x_copy(k).start()
        elif op == "M":
            for i in range(1, n):
                meta_copy(i).wait_recv()
            meta_cross.start()
            meta_cross.wait_recv()
            to_smem = pltpu.make_async_copy(meta_in, meta_s, m_copy)
            to_smem.start()
            to_smem.wait()
        elif op == "W":
            bias_copy.wait()
            for i in range(chip_blocks):
                bias[i] = bias_in[:, i * tile:(i + 1) * tile]
            w_local.wait()
            w_arrives.wait_recv()
        elif op == "C":
            x_copy(k).wait_recv()
            compute(k)
            b_copy(k).start()
        else:
            b_copy(k).wait_recv()
            mine = facts(0, k)[0] == plane
            for j in range(CAP):
                sel[k, j] = jnp.where(mine, ores[k, j], xres[k, j])
            if k:
                f_copy(k).start()

    for j in range(CAP):
        fin[0, j] = sel[0, j]
    for k in range(1, n):
        f_copy(k).wait_recv()
    for p in range(live):
        block = demand_ref[0, p]
        k = lax.bitwise_xor(lax.div(block, per_range), r)
        out_ref[:, p * tile:(p + 1) * tile] = fin[k, lax.rem(block, CAP)]

    for k in range(n):
        if k:
            meta_copy(k).wait_send()
            z_copy(k).wait_send()
            f_copy(k).wait_send()
        x_copy(k).wait_send()
        b_copy(k).wait_send()
    meta_cross.wait_send()
    w_remote.wait_send()


def fused_shards(activations, weight_tiles, tile_index, bias_terms, demand):
    n = lax.axis_size("rows")
    layers, held, kinds, tile, _ = weight_tiles.shape
    depth = activations.shape[0]
    chip_blocks = held * CORES
    weights = weight_tiles.reshape(layers, held, kinds * tile, tile)
    smem = pl.BlockSpec(memory_space=pltpu.SMEM)
    vmem = pl.BlockSpec(memory_space=pltpu.VMEM)
    hbm = pl.BlockSpec(memory_space=pltpu.HBM)
    slot = pltpu.VMEM((n, CAP, depth, tile), jnp.bfloat16)
    single = [pltpu.VMEM((CAP, depth, tile), jnp.bfloat16)] * n
    state = pltpu.VMEM((2, CAP, depth, tile), jnp.bfloat16)
    sems = pltpu.SemaphoreType.DMA((n,))
    return pl.pallas_call(
        functools.partial(fused_kernel, n),
        out_shape=jax.ShapeDtypeStruct(activations.shape, jnp.bfloat16),
        in_specs=[smem, smem, hbm, hbm, hbm],
        out_specs=vmem,
        scratch_shapes=[
            pltpu.VMEM((demand.shape[1], depth, tile), jnp.bfloat16),
            pltpu.VMEM((layers, chip_blocks * tile), jnp.float32),
            pltpu.VMEM((chip_blocks, layers, tile), jnp.float32),
            pltpu.VMEM((CORES, layers, held, kinds * tile, tile), jnp.bfloat16),
            slot, single, single, slot, slot, slot, slot, slot, state, state,
            pltpu.VMEM((1, 128), jnp.int32),
            pltpu.VMEM((2, n, 1, 128), jnp.int32),
            pltpu.SMEM((2, n, 1, 128), jnp.int32),
            pltpu.SemaphoreType.DMA((2,)),
            pltpu.SemaphoreType.DMA((3,)),
            sems, sems,
            pltpu.SemaphoreType.DMA((2,)),
            pltpu.SemaphoreType.DMA,
            sems, sems, sems, sems, sems, sems, sems, sems,
        ],
        compiler_params=pltpu.CompilerParams(
            collective_id=0, has_side_effects=True, vmem_limit_bytes=44 * 1024 * 1024
        ),
    )(*[
        pltpu.with_memory_space_constraint(operand, pltpu.HBM)
        for operand in (demand, tile_index.transpose(0, 2, 1), activations, bias_terms, weights)
    ])


def solution(mesh):
    rows, grp = mesh.shape["rows"], mesh.shape["grp"]

    def shards(activations, weight_tiles, tile_index, bias_terms, demand):
        held, kinds = weight_tiles.shape[1], weight_tiles.shape[2]
        fits = rows == 8 and grp == PLANES * CORES and held * grp <= 16 * CAP
        fits = fits and demand.shape[1] <= 16 and demand.shape[1] % CAP == 0
        if fits and held % CAP == 0 and kinds == 2:
            return fused_shards(activations, weight_tiles, tile_index, bias_terms, demand)
        return gathered_shards(activations, weight_tiles, tile_index, bias_terms, demand)

    return jax.shard_map(
        shards,
        mesh=mesh,
        in_specs=(
            P(("rows", "grp"), None),
            P(None, ("rows", "grp"), None, None, None),
            P(),
            P(),
            P(("rows", "grp"), None),
        ),
        out_specs=P(("rows", "grp"), None),
        check_vma=False,
    )
```

time: 64 us -> 55.7 us (0.87)
  local copies, waits for them, and re-layouts: 4.81 us -> 0.75 us
  Pallas kernels: 57.2 us -> 54.1 us
  other arithmetic: 1.74 us -> 0 us
    pallas_call x1, Pallas kernels: 57.2 us -> 54.1 us  [fused_shards(): pl.pallas_call(functools.partial(fused_kernel, n), out_shape=jax.ShapeDty...]
    unnamed x5 -> x1, local copies, waits for them, and re-layouts: 2.64 us -> 0.75 us
    select_n x4 -> x0, other arithmetic: 1.36 us -> none  [the longest x1 0.67 us: fused_shards(): blocks % per_range]
    transpose x1 -> x0, local copies, waits for them, and re-layouts: 1.07 us -> none  [fused_shards(): activations.reshape(depth, blocks.shape[0], tile).transpose(1, 0, 2)]
    dynamic_slice x2 -> x0, local copies, waits for them, and re-layouts: 0.86 us -> none  [the longest x1 0.84 us: fused_shards(): lax.dynamic_slice_in_dim(tile_index[:, :, 0], chip, chip_blocks, axis=1)]
where the time goes in v1:
time: 55.7 us; the launch traced here: 54.9 us
  Pallas kernels  54.1 us (97%)
  local copies, waits for them, and re-layouts  0.75 us (1%)
    pallas_call x1, Pallas kernels, fused_shards(): pl.pallas_call(functools.partial(fused_kernel, n), out_shape=jax.ShapeDty...  54.1 us

profile of v1, /device:TPU:0, one launch (start us, length us, event | category | flops | bytes accessed | tf_op | source)
XLA Modules:
  0.0 54.9 jit_solution(1798421616715472285)
XLA Ops:
  0.0 54.1 %shard_map.55 = bf16[96,2048]{1,0:T(8,128)(2,1)S(1)} custom-call(s32[1,16]{1,0:T(1,128)} %demand_ref.1, s32[3,1,512]{2,1,0:T(1,128)} %bitcast.3, bf16[96,2048]{1,0:T(8,128)(2,1)} %act_hbm.1, f32[3,65536]{1,0:T(4,128)} %bias_hbm.1, bf16[3,16,256,128]{3,2,1,0:T(8,128)(2,1)} %bitcast.2), custom_call_target="tpu_custom_call" | custom-call | tf_op jit(solution)/shard_map/pallas_call | solution.py:294
  54.1 0.7 %copy.7 = bf16[96,2048]{1,0:T(8,128)(2,1)} copy(bf16[96,2048]{1,0:T(8,128)(2,1)S(1)} %shard_map.55) | data formatting | bytes 786432

commit v2 on v1

--- a/solution.py
+++ b/solution.py
@@ -10,7 +10,7 @@
 CAP = 4
 CORES = 2
 PLANES = 2
-SENDS = (1, 2, 3, 6, 4, 7, 5)
+
 MESH = pl.DeviceIdType.MESH
 
 
@@ -67,13 +67,17 @@
     return current.reshape(current.shape[0], live_count * tile_width)
 
 
-SCHEDULE = "F1 F2 F3 M W C0 C1 F4 C2 C3 R0 F5 R1 C4 R2 F6 R3 C5 F7 C6 R4 C7 R5 R6 R7"
+SCHEDULE = (
+    "F1", "F2", "F4", "W", "C0", "F3", "C4", "B4", "F5", "C1", "C2",
+    "F6", "R4", "C3", "C5", "B5", "C6", "B2", "F7", "B6", "R5", "C7",
+    "B7", "R6", "B3", "B1", "B0", "R2", "R7", "R3", "R1", "R0",
+)
 
 
 def fused_kernel(
-    n, demand_ref, index_ref, act_hbm, bias_hbm, w_hbm, out_ref,
-    act, bias_in, bias, w_all, slots, zin, xin, ores, fres, xres, sel, fin, st_own, st_for,
-    meta_out, meta_in, meta_s, in_sems, w_sems, m_send, m_recv, mx_sems, m_copy,
+    n, demand_hbm, index_hbm, act_hbm, bias_hbm, w_hbm, out_ref,
+    demand_ref, index_ref, act, bias_in, bias, w_all, slots, zin, xin, ores, fres, xres, sel, fin,
+    st_own, st_for, meta_s, in_sems, w_sems, tokens, m_send, m_recv, mx_send, mx_recv,
     z_send, z_recv, x_send, x_recv, b_send, b_recv, f_send, f_recv,
 ):
     layers, held = w_hbm.shape[0], w_hbm.shape[1]
@@ -87,25 +91,39 @@
     mate = plane * CORES + (CORES - 1 - core)
     cross = (PLANES - 1 - plane) * CORES + core
     bits = n.bit_length() - 1
+    inner_z = (r // 2 + 1) // 2 % 2
 
     def peer(k):
         row = 0
         for b in range(bits):
-            row = row + ((r // (1 << b)) % 2 + (k >> b)) % 2 * (1 << b)
+            row = row + ((r // (1 << b)) % 2 + (k // (1 << b)) % 2) % 2 * (1 << b)
         return row
 
     peers = [peer(k) for k in range(n)]
+    labels = list(range(5)) + [6 - inner_z, 7 - inner_z, 5 + 2 * inner_z]
+
+    def greet(sem):
+        pl.semaphore_signal(sem, inc=1, device_id=(peers[2], g), device_id_type=MESH)
+
+        @pl.when(inner_z == 1)
+        def _():
+            pl.semaphore_signal(sem, inc=1, device_id=(peers[6], g), device_id_type=MESH)
+
     barrier = pltpu.get_barrier_semaphore()
-    for k in range(n - 1, 0, -1):
-        pl.semaphore_signal(barrier, inc=1, device_id=(peers[k], g), device_id_type=MESH)
+    greet(barrier)
+    pl.semaphore_signal(barrier, inc=1, device_id=(peers[1], g), device_id_type=MESH)
     pl.semaphore_signal(barrier, inc=1, device_id=(r, cross), device_id_type=MESH)
     pl.semaphore_signal(barrier, inc=1, device_id=(r, mate), device_id_type=MESH)
 
+    demand_copy = pltpu.make_async_copy(demand_hbm, demand_ref, in_sems.at[2])
+    demand_copy.start()
     for p in range(live):
         pltpu.make_async_copy(
             act_hbm.at[:, pl.ds(p * tile, tile)], act.at[p], in_sems.at[0]
         ).start()
     act_copy = pltpu.make_async_copy(act, act, in_sems.at[0])
+    index_copy = pltpu.make_async_copy(index_hbm, index_ref, in_sems.at[3])
+    index_copy.start()
     first = (r * PLANES + plane) * chip_blocks
     bias_copy = pltpu.make_async_copy(
         bias_hbm.at[:, pl.ds(pl.multiple_of(first * tile, tile), chip_blocks * tile)],
@@ -115,6 +133,15 @@
     w_local = pltpu.make_async_copy(w_hbm, w_all.at[core], w_sems.at[0])
     w_local.start()
 
+    pl.semaphore_wait(barrier, 4 + inner_z)
+    greet(tokens.at[0])
+    w_remote = pltpu.make_async_remote_copy(
+        src_ref=w_hbm, dst_ref=w_all.at[core],
+        send_sem=w_sems.at[1], recv_sem=w_sems.at[2],
+        device_id=(r, mate), device_id_type=MESH,
+    )
+    w_remote.start()
+    demand_copy.wait()
     places = [jnp.int32(0)] * CAP
     groups = jnp.int32(0)
     for p in range(live):
@@ -128,39 +155,49 @@
             places[c] = places[c] + jnp.where(member == c, p * scale, 0)
         group = lax.div(lax.rem(block, per_range), CAP)
         groups = groups + jnp.where(member == 0, group * scale, 0)
-    meta_out[...] = jnp.full(meta_out.shape, groups, jnp.int32)
-    meta_in[0, 0] = jnp.full(meta_out.shape, groups, jnp.int32)
+    for k in range(n):
+        meta_s[0, k, 0, 0] = groups
     act_copy.wait()
-    for k in range(n - 1, -1, -1):
+
+    def build(k):
         for c in range(CAP):
             pos = lax.bitwise_and(lax.shift_right_logical(places[c], peers[k] * 4), 15)
             slots[k, c] = act[pos]
 
-    pl.semaphore_wait(barrier, n + 1)
-
     def meta_copy(k):
         return pltpu.make_async_remote_copy(
-            src_ref=meta_out, dst_ref=meta_in.at[0, k],
+            src_ref=meta_s.at[0, 0], dst_ref=meta_s.at[1, k],
             send_sem=m_send.at[k], recv_sem=m_recv.at[k],
             device_id=(peers[k], g), device_id_type=MESH,
         )
 
-    meta_cross = pltpu.make_async_remote_copy(
-        src_ref=meta_in.at[0], dst_ref=meta_in.at[1],
-        send_sem=mx_sems.at[0], recv_sem=mx_sems.at[1],
-        device_id=(r, cross), device_id_type=MESH,
-    )
+    def z_arrives(i):
+        k = labels[i]
+        for src, dst, sem in ((meta_s.at[0, 0], meta_s.at[1, k], m_recv), (slots.at[i], zin.at[k], z_recv)):
+            pltpu.make_async_remote_copy(
+                src_ref=src, dst_ref=dst, send_sem=z_send.at[i], recv_sem=sem.at[k],
+                device_id=(peers[i], g), device_id_type=MESH,
+            ).wait_recv()
+            if sem is m_recv:
+                mx_copy(i).start()
+
+    def mx_copy(k):
+        return pltpu.make_async_remote_copy(
+            src_ref=meta_s.at[1 if k else 0, labels[k]], dst_ref=meta_s.at[2, k],
+            send_sem=mx_send.at[k], recv_sem=mx_recv.at[k],
+            device_id=(r, cross), device_id_type=MESH,
+        )
 
     def z_copy(k):
         return pltpu.make_async_remote_copy(
-            src_ref=slots.at[k], dst_ref=zin[k],
+            src_ref=slots.at[k], dst_ref=zin.at[k],
             send_sem=z_send.at[k], recv_sem=z_recv.at[k],
             device_id=(peers[k], g), device_id_type=MESH,
         )
 
     def x_copy(k):
         return pltpu.make_async_remote_copy(
-            src_ref=zin[k] if k else slots.at[0], dst_ref=xin[k],
+            src_ref=zin.at[labels[k]] if k else slots.at[0], dst_ref=xin[k],
             send_sem=x_send.at[k], recv_sem=x_recv.at[k],
             device_id=(r, cross), device_id_type=MESH,
         )
@@ -174,46 +211,71 @@
 
     def f_copy(k):
         return pltpu.make_async_remote_copy(
-            src_ref=sel.at[k], dst_ref=fin.at[k],
-            send_sem=f_send.at[k], recv_sem=f_recv.at[k],
-            device_id=(peers[k], g), device_id_type=MESH,
-        )
-
-    w_remote = pltpu.make_async_remote_copy(
-        src_ref=w_hbm, dst_ref=w_all.at[core],
-        send_sem=w_sems.at[1], recv_sem=w_sems.at[2],
-        device_id=(r, mate), device_id_type=MESH,
-    )
+            src_ref=sel.at[k], dst_ref=fin.at[labels[k]],
+            send_sem=f_send.at[k], recv_sem=f_recv.at[labels[k]],
+            device_id=(peer(labels[k]), g), device_id_type=MESH,
+        )
+
     w_arrives = pltpu.make_async_remote_copy(
         src_ref=w_hbm, dst_ref=w_all.at[CORES - 1 - core],
         send_sem=w_sems.at[1], recv_sem=w_sems.at[2],
         device_id=(r, mate), device_id_type=MESH,
     )
 
-    for k in SENDS:
+    def send(k):
         meta_copy(k).start()
+        z_copy(k).start()
+
+    def send_if(where, k):
+        @pl.when(inner_z == where)
+        def _():
+            send(k)
+
+    def heard(i):
+        pl.semaphore_wait(tokens.at[i], 1 + inner_z)
+
+    build(0)
+    mx_copy(0).start()
     x_copy(0).start()
-    for k in SENDS:
-        z_copy(k).start()
-    w_remote.start()
+    build(1)
+    send(1)
+    heard(0)
+    greet(tokens.at[1])
+    build(2)
+    send(2)
+    build(4)
+    send(4)
+    build(3)
+    send(3)
+    build(5)
+    build(6)
+    heard(1)
+    greet(tokens.at[2])
+    send(6)
+    send(5)
+    build(7)
+    send_if(1, 7)
+    heard(2)
+    send_if(0, 7)
 
     def facts(which, k):
-        group = lax.bitwise_and(lax.shift_right_logical(meta_s[which, k, 0, 0], r * 4), 15)
+        group = lax.bitwise_and(lax.shift_right_logical(meta_s[which if k or which == 2 else 0, k if which == 2 else labels[k], 0, 0], r * 4), 15)
         within = group * CAP
         half = lax.rem(within, chip_blocks) // held
         return lax.div(within, chip_blocks), half, lax.rem(within, held), lax.rem(within, chip_blocks)
 
     def compute(k):
-        near = zin[k] if k else slots.at[0]
+        for j in range(CAP):
+            st_own[0, j] = zin[labels[k], j] if k else slots[0, j]
         jobs = []
-        for which, load, store, state in ((1, xin[k], fres, st_for), (0, near, ores, st_own)):
+        for which, load, store, state in ((2, xin[k], fres, st_for), (1, None, ores, st_own)):
             _, half, local, inner = facts(which, k)
             jobs.append((load, store, state, half, local, inner))
         for layer in range(layers):
             for load, store, state, half, local, inner in jobs:
                 for j in range(CAP):
                     other = lax.rem(index_ref[layer, 0, first + inner + j], CAP)
-                    if layer == 0:
+                    if layer == 0 and load is not None:
                         pair = (load[j], load[other])
                     else:
                         pair = (state[layer % 2, j], state[layer % 2, other])
@@ -227,32 +289,27 @@
                     else:
                         state[(layer + 1) % 2, j] = value
 
-    for token in SCHEDULE.split():
+    for token in SCHEDULE:
         op, k = token[0], int(token[1:] or 0)
         if op == "F":
-            z_copy(k).wait_recv()
+            z_arrives(k)
             x_copy(k).start()
-        elif op == "M":
-            for i in range(1, n):
-                meta_copy(i).wait_recv()
-            meta_cross.start()
-            meta_cross.wait_recv()
-            to_smem = pltpu.make_async_copy(meta_in, meta_s, m_copy)
-            to_smem.start()
-            to_smem.wait()
         elif op == "W":
+            index_copy.wait()
             bias_copy.wait()
             for i in range(chip_blocks):
                 bias[i] = bias_in[:, i * tile:(i + 1) * tile]
             w_local.wait()
             w_arrives.wait_recv()
         elif op == "C":
+            mx_copy(k).wait_recv()
             x_copy(k).wait_recv()
             compute(k)
+        elif op == "B":
             b_copy(k).start()
         else:
             b_copy(k).wait_recv()
-            mine = facts(0, k)[0] == plane
+            mine = facts(1, k)[0] == plane
             for j in range(CAP):
                 sel[k, j] = jnp.where(mine, ores[k, j], xres[k, j])
             if k:
@@ -272,9 +329,9 @@
             meta_copy(k).wait_send()
             z_copy(k).wait_send()
             f_copy(k).wait_send()
+        mx_copy(k).wait_send()
         x_copy(k).wait_send()
         b_copy(k).wait_send()
-    meta_cross.wait_send()
     w_remote.wait_send()
 
 
@@ -284,7 +341,6 @@
     depth = activations.shape[0]
     chip_blocks = held * CORES
     weights = weight_tiles.reshape(layers, held, kinds * tile, tile)
-    smem = pl.BlockSpec(memory_space=pltpu.SMEM)
     vmem = pl.BlockSpec(memory_space=pltpu.VMEM)
     hbm = pl.BlockSpec(memory_space=pltpu.HBM)
     slot = pltpu.VMEM((n, CAP, depth, tile), jnp.bfloat16)
@@ -294,22 +350,21 @@
     return pl.pallas_call(
         functools.partial(fused_kernel, n),
         out_shape=jax.ShapeDtypeStruct(activations.shape, jnp.bfloat16),
-        in_specs=[smem, smem, hbm, hbm, hbm],
+        in_specs=[hbm] * 5,
         out_specs=vmem,
         scratch_shapes=[
+            pltpu.SMEM(demand.shape, jnp.int32),
+            pltpu.SMEM((layers, 1, tile_index.shape[1]), jnp.int32),
             pltpu.VMEM((demand.shape[1], depth, tile), jnp.bfloat16),
             pltpu.VMEM((layers, chip_blocks * tile), jnp.float32),
             pltpu.VMEM((chip_blocks, layers, tile), jnp.float32),
             pltpu.VMEM((CORES, layers, held, kinds * tile, tile), jnp.bfloat16),
-            slot, single, single, slot, slot, slot, slot, slot, state, state,
-            pltpu.VMEM((1, 128), jnp.int32),
-            pltpu.VMEM((2, n, 1, 128), jnp.int32),
-            pltpu.SMEM((2, n, 1, 128), jnp.int32),
-            pltpu.SemaphoreType.DMA((2,)),
+            slot, slot, single, slot, slot, slot, slot, slot, state, state,
+            pltpu.SMEM((3, n, 1, 128), jnp.int32),
+            pltpu.SemaphoreType.DMA((4,)),
             pltpu.SemaphoreType.DMA((3,)),
-            sems, sems,
-            pltpu.SemaphoreType.DMA((2,)),
-            pltpu.SemaphoreType.DMA,
+            pltpu.SemaphoreType.REGULAR((3,)),
+            sems, sems, sems, sems,
             sems, sems, sems, sems, sems, sems, sems, sems,
         ],
         compiler_params=pltpu.CompilerParams(

time: 55.7 us -> 46.9 us (0.84); the launches traced: 54.9 us -> 46.7 us
  Pallas kernels: 54.1 us -> 45.9 us
    pallas_call x1, Pallas kernels: 54.1 us -> 45.9 us  [fused_shards(): pl.pallas_call(functools.partial(fused_kernel, n), out_shape=jax.ShapeDty...]
where the time goes in v2:
time: 46.9 us; the launch traced here: 46.7 us
  Pallas kernels  45.9 us (98%)
  local copies, waits for them, and re-layouts  0.75 us (2%)
    pallas_call x1, Pallas kernels, fused_shards(): pl.pallas_call(functools.partial(fused_kernel, n), out_shape=jax.ShapeDty...  45.9 us

profile of v2, /device:TPU:0, one launch (start us, length us, event | category | flops | bytes accessed | tf_op | source)
XLA Modules:
  0.0 46.7 jit_solution(4716324575861656276)
XLA Ops:
  0.0 45.9 %shard_map.55 = bf16[96,2048]{1,0:T(8,128)(2,1)S(1)} custom-call(s32[1,16]{1,0:T(1,128)} %demand_hbm.1, s32[3,1,512]{2,1,0:T(1,128)} %bitcast.3, bf16[96,2048]{1,0:T(8,128)(2,1)} %act_hbm.1, f32[3,65536]{1,0:T(4,128)} %bias_hbm.1, bf16[3,16,256,128]{3,2,1,0:T(8,128)(2,1)} %bitcast.2), custom_call_target="tpu_custom_call" | custom-call | tf_op jit(solution)/shard_map/pallas_call | solution.py:350
  46.0 0.7 %copy.7 = bf16[96,2048]{1,0:T(8,128)(2,1)} copy(bf16[96,2048]{1,0:T(8,128)(2,1)S(1)} %shard_map.55) | data formatting | bytes 786432

commit v3 on v2

--- a/solution.py
+++ b/solution.py
@@ -10,7 +10,6 @@
 CAP = 4
 CORES = 2
 PLANES = 2
-
 MESH = pl.DeviceIdType.MESH
 
 
@@ -68,9 +67,9 @@
 
 
 SCHEDULE = (
-    "F1", "F2", "F4", "W", "C0", "F3", "C4", "B4", "F5", "C1", "C2",
-    "F6", "R4", "C3", "C5", "B5", "C6", "B2", "F7", "B6", "R5", "C7",
-    "B7", "R6", "B3", "B1", "B0", "R2", "R7", "R3", "R1", "R0",
+    "F1", "F2", "F4", "W", "F3", "C0", "C4", "B4", "C1", "F5", "C2",
+    "F6", "C3", "C5", "B5", "R4", "B2", "F7", "R5", "C6", "B6", "C7",
+    "B3", "B7", "B1", "R6", "B0", "R7", "R3", "R1", "R2", "R0",
 )
 
 

time: 46.9 us -> 46.7 us (level)
  no operation moved by 1% of the time
where the time goes in v3:
time: 46.7 us; the launch traced here: 46.5 us
  Pallas kernels  45.8 us (98%)
  local copies, waits for them, and re-layouts  0.75 us (2%)
    pallas_call x1, Pallas kernels, fused_shards(): pl.pallas_call(functools.partial(fused_kernel, n), out_shape=jax.ShapeDty...  45.8 us

profile of v3, /device:TPU:0, one launch (start us, length us, event | category | flops | bytes accessed | tf_op | source)
XLA Modules:
  0.0 46.5 jit_solution(3270900570372695699)
XLA Ops:
  0.0 45.8 %shard_map.55 = bf16[96,2048]{1,0:T(8,128)(2,1)S(1)} custom-call(s32[1,16]{1,0:T(1,128)} %demand_hbm.1, s32[3,1,512]{2,1,0:T(1,128)} %bitcast.3, bf16[96,2048]{1,0:T(8,128)(2,1)} %act_hbm.1, f32[3,65536]{1,0:T(4,128)} %bias_hbm.1, bf16[3,16,256,128]{3,2,1,0:T(8,128)(2,1)} %bitcast.2), custom_call_target="tpu_custom_call" | custom-call | tf_op jit(solution)/shard_map/pallas_call | solution.py:349
  45.8 0.7 %copy.7 = bf16[96,2048]{1,0:T(8,128)(2,1)} copy(bf16[96,2048]{1,0:T(8,128)(2,1)S(1)} %shard_map.55) | data formatting | bytes 786432

commit v4 on v3

--- a/solution.py
+++ b/solution.py
@@ -310,12 +310,10 @@
             b_copy(k).wait_recv()
             mine = facts(1, k)[0] == plane
             for j in range(CAP):
-                sel[k, j] = jnp.where(mine, ores[k, j], xres[k, j])
+                (sel if k else fin)[k, j] = jnp.where(mine, ores[k, j], xres[k, j])
             if k:
                 f_copy(k).start()
 
-    for j in range(CAP):
-        fin[0, j] = sel[0, j]
     for k in range(1, n):
         f_copy(k).wait_recv()
     for p in range(live):

time: 46.7 us -> 46.7 us (level)
  no operation moved by 1% of the time
where the time goes in v4:
time: 46.7 us; the launch traced here: 46.5 us
  Pallas kernels  45.8 us (98%)
  local copies, waits for them, and re-layouts  0.75 us (2%)
    pallas_call x1, Pallas kernels, fused_shards(): pl.pallas_call(functools.partial(fused_kernel, n), out_shape=jax.ShapeDty...  45.8 us

profile of v4, /device:TPU:0, one launch (start us, length us, event | category | flops | bytes accessed | tf_op | source)
XLA Modules:
  0.0 46.5 jit_solution(5861198564994742097)
XLA Ops:
  0.0 45.8 %shard_map.55 = bf16[96,2048]{1,0:T(8,128)(2,1)S(1)} custom-call(s32[1,16]{1,0:T(1,128)} %demand_hbm.1, s32[3,1,512]{2,1,0:T(1,128)} %bitcast.3, bf16[96,2048]{1,0:T(8,128)(2,1)} %act_hbm.1, f32[3,65536]{1,0:T(4,128)} %bias_hbm.1, bf16[3,16,256,128]{3,2,1,0:T(8,128)(2,1)} %bitcast.2), custom_call_target="tpu_custom_call" | custom-call | tf_op jit(solution)/shard_map/pallas_call | solution.py:347
  45.8 0.7 %copy.7 = bf16[96,2048]{1,0:T(8,128)(2,1)} copy(bf16[96,2048]{1,0:T(8,128)(2,1)S(1)} %shard_map.55) | data formatting | bytes 786432
